TPU v7x, 32 devices: a whole 2x2x4 slice. The times are simulated.
32 devices in a mesh: comp: 2 (over core), lat: 4 (over z), lon: 4 (over y, x).
Axes of the slice: x: 2, y: 2, z: 4, core: 2. Of those that a mesh axis runs over, the one named last changes fastest.
Arguments:
- fields: float32 [2, 7, 2048, 256], P('comp', None, ('lat', 'lon')), may hold values from -4 to 4, as said below
- block_owner: int32 [2048], P(('lat', 'lon')), may hold values from 0 to 2047, as said below
- ice_covered: int32 [2048], P(('lat', 'lon')), may hold values 0 or 1
- land_mask: int32 [2048, 256], P(('lat', 'lon')), may hold values 0 or 1
Outputs:
- coupled_out: float32 [2, 2, 2048, 256], P('comp', None, ('lat', 'lon'))
Inputs may be any that keep to these rules, and one draw needn't show every extreme that they name: `block_owner`: every block id appears once. Slot d of lat+lon index o holds a block of the ice tile of index d, that is an id from d * 128 to d * 128 + 127. `fields`: ocean channels: winds within 4, currents within 1.5, tilts within 1, air density 0.9 to 1.3; ice channels: velocities within 1.5, mass 0.5 to 4, concentration 0.05 to 1, stresses within 1.5.
All inputs are finite; a program needn't handle non-finite values.
Results may differ from a plain program's by a relative error of at most 0.00002.
Values sent between devices are 32-bit elements.
A program may use at most 64 MiB of HBM per device.

v0:
```python
import jax
import jax.numpy as jnp
from jax import lax
from jax.sharding import PartitionSpec as P

GX = 1
BY = 2
BX = 128
NSUB = 4


CD_ICE = 0.1
CW = 1.5
CSTAR = 2.0
ECC2 = 4.0
DMIN2 = 0.25
RELAX = 0.5
DTE = 0.5
CORIO = 0.3
MASS_FLOOR = 0.5
DRAG_FLOOR = 0.1


def from_behind(x, axis, by):
    size = lax.axis_size(axis)
    pairs = [(i, i + by) for i in range(size) if 0 <= i + by < size]
    return lax.ppermute(x, axis, pairs)


def with_halo(x, sides, width, wrap):
    for axis, dim in sides:
        size, length = (lax.axis_size(axis), x.shape[dim])
        up = [(i, (i + 1) % size) for i in range(size if wrap else size - 1)]
        down = [(j, i) for i, j in up]
        last = lax.slice_in_dim(x, length - width, length, axis=dim)
        first = lax.slice_in_dim(x, 0, width, axis=dim)
        before = lax.ppermute(last, axis, up)
        after = lax.ppermute(first, axis, down)
        x = jnp.concatenate([before, x, after], axis=dim)
    return x


def air_stress(ocean):
    wind_x, wind_y, current_x, current_y, tilt_x, tilt_y, density = ocean
    speed_ice = jnp.sqrt(wind_x * wind_x + wind_y * wind_y + 1.0)
    scale_ice = density * CD_ICE * speed_ice
    rel_x = wind_x - current_x
    rel_y = wind_y - current_y
    speed_open = jnp.sqrt(rel_x * rel_x + rel_y * rel_y + 1.0)
    scale_open = density * (0.1 + 0.05 * speed_open) * speed_open
    outbound = jnp.stack(
        [scale_ice * wind_x, scale_ice * wind_y, current_x, current_y, tilt_x, tilt_y]
    )
    open_stress = jnp.stack([scale_open * rel_x, scale_open * rel_y])
    return (outbound, open_stress)


def prepare(ice_tile, forcing, active):
    ice_mass = ice_tile[2]
    concentration = ice_tile[3]
    strength = ice_mass * jnp.exp(CSTAR * (concentration - 1.0)) * active
    drag_base = CW * concentration * active
    push_x = active * (concentration * forcing[0] - ice_mass * forcing[4])
    push_y = active * (concentration * forcing[1] - ice_mass * forcing[5])
    return jnp.stack(
        [strength, ice_mass, drag_base, push_x, push_y, forcing[2], forcing[3], active]
    )


def subcycle(ice_state, statics):
    east_vel, north_vel, stress_one, stress_two, stress_three = ice_state
    strength = statics[0]
    east_base = east_vel[:-1, :-1]
    north_base = north_vel[:-1, :-1]
    strain_xx = east_vel[:-1, 1:] - east_base
    strain_yy = north_vel[1:, :-1] - north_base
    shear = east_vel[1:, :-1] - east_base + (north_vel[:-1, 1:] - north_base)
    divergence = strain_xx + strain_yy
    tension = strain_xx - strain_yy
    delta_norm = jnp.sqrt(
        divergence * divergence + (tension * tension + shear * shear) / ECC2 + DMIN2
    )
    viscosity = strength[:-1, :-1] / delta_norm
    stress_sum = (stress_one[:-1, :-1] + RELAX * viscosity * (divergence - delta_norm)) / (
        1.0 + RELAX
    )
    stress_diff = (stress_two[:-1, :-1] + RELAX * viscosity * tension / ECC2) / (1.0 + RELAX)
    stress_shear = (stress_three[:-1, :-1] + RELAX * viscosity * shear / (2.0 * ECC2)) / (
        1.0 + RELAX
    )
    stress_xx = 0.5 * (stress_sum + stress_diff)
    stress_yy = 0.5 * (stress_sum - stress_diff)
    force_x = (
        stress_xx[1:, 1:] - stress_xx[1:, :-1] + (stress_shear[1:, 1:] - stress_shear[:-1, 1:])
    )
    force_y = (
        stress_shear[1:, 1:] - stress_shear[1:, :-1] + (stress_yy[1:, 1:] - stress_yy[:-1, 1:])
    )
    trimmed = statics[:, 1:-1, 1:-1]
    strength, ice_mass, drag_base, push_x, push_y, current_x, current_y, active = trimmed
    east_old = east_vel[1:-1, 1:-1]
    north_old = north_vel[1:-1, 1:-1]
    diff_x = current_x - east_old
    diff_y = current_y - north_old
    drag_coef = drag_base * jnp.sqrt(diff_x * diff_x + diff_y * diff_y + DRAG_FLOOR)
    denominator = jnp.maximum(ice_mass, MASS_FLOOR) / DTE + drag_coef
    east_new = (
        active
        * (
            ice_mass / DTE * east_old
            + force_x
            + push_x
            + drag_coef * current_x
            + CORIO * ice_mass * north_old
        )
        / denominator
    )
    north_new = (
        active
        * (
            ice_mass / DTE * north_old
            + force_y
            + push_y
            + drag_coef * current_y
            - CORIO * ice_mass * east_old
        )
        / denominator
    )
    new_state = jnp.stack(
        [east_new, north_new, stress_sum[1:, 1:], stress_diff[1:, 1:], stress_shear[1:, 1:]]
    )
    return (new_state, trimmed)


def give_back(ice_state, statics):
    east_vel = ice_state[0]
    north_vel = ice_state[1]
    drag_base = statics[2]
    current_x = statics[5]
    current_y = statics[6]
    diff_x = east_vel - current_x
    diff_y = north_vel - current_y
    factor = drag_base * jnp.sqrt(diff_x * diff_x + diff_y * diff_y + DRAG_FLOOR)
    return jnp.stack([factor * diff_x, factor * diff_y, drag_base / CW])


def to_tile(blocks):
    channels, count, cells = blocks.shape
    arranged = blocks.reshape(channels, count // GX, GX, BY, BX).transpose(0, 1, 3, 2, 4)
    return arranged.reshape(channels, count // GX * BY, GX * BX)


def from_tile(values):
    channels, rows, columns = values.shape
    arranged = values.reshape(channels, rows // BY, BY, GX, BX).transpose(0, 1, 3, 2, 4)
    return arranged.reshape(channels, rows // BY * GX, BY * BX)


def per_device(fields, block_owner, ice_covered, land_mask):
    count = block_owner.shape[0]
    is_ocean = lax.axis_index("comp") == 0
    outbound, open_stress = air_stress(fields[0])
    owner_row = block_owner.reshape(1, count)
    crossed = from_behind(outbound, "comp", 1)
    received, anchor = (
        lax.all_to_all(crossed, ("lat", "lon"), split_axis=1, concat_axis=1, tiled=True),
        lax.all_to_all(owner_row, ("lat", "lon"), split_axis=1, concat_axis=1, tiled=True),
    )
    local_ids = anchor[0] % count
    position = jnp.zeros((count,), jnp.int32).at[local_ids].set(jnp.arange(count, dtype=jnp.int32))
    forcing = to_tile(received[:, position])
    ice_tile = to_tile(fields[0])
    covered = ice_covered.astype(jnp.float32)[:, None] * (1 - land_mask).astype(jnp.float32)
    active = to_tile(covered[None])[0]
    statics = prepare(ice_tile, forcing, active)
    ice_state = jnp.stack([ice_tile[0], ice_tile[1], ice_tile[4], ice_tile[5], ice_tile[6]])
    joined = jnp.concatenate([ice_state, statics], 0)
    joined = with_halo(joined, (("lon", 2),), NSUB, True)
    joined = with_halo(joined, (("lat", 1),), NSUB, False)
    ice_state = joined[:5]
    statics = joined[5:]
    for repeat in range(NSUB):
        ice_state, statics = subcycle(ice_state, statics)
    returned = from_tile(give_back(ice_state, statics))
    back_send = returned[:, local_ids]
    regrouped = lax.all_to_all(back_send, ("lat", "lon"), split_axis=1, concat_axis=1, tiled=True)
    received_back = from_behind(regrouped, "comp", -1)
    ocean_out = received_back[:2] + (1.0 - received_back[2]) * open_stress
    ice_out = from_tile(ice_state[:2])
    return jnp.where(is_ocean, ocean_out, ice_out)[None]


def solution(mesh):
    placed = (
        P("comp", None, ("lat", "lon"), None),
        P(("lat", "lon")),
        P(("lat", "lon")),
        P(("lat", "lon"), None),
    )
    return jax.shard_map(
        per_device,
        mesh=mesh,
        in_specs=placed,
        out_specs=P("comp", None, ("lat", "lon"), None),
        check_vma=False,
    )
```

profile of v0, /device:TPU:0, one launch (start us, length us, event | category | flops | bytes accessed | tf_op | source)
XLA Modules:
  0.0 125.6 jit_solution(1248778814458722191)
XLA Ops:
  0.0 1.8 %fusion.89 = f32[6,128,256]{2,1,0:T(8,128)} fusion(f32[1,7,128,256]{3,2,1,0:T(8,128)} %param.4), kind=kLoop, calls=%fused_computation.211 | loop fusion | flops 229375 | bytes 524288
  1.8 1.8 %fusion.88 = f32[6,128,256]{2,1,0:T(8,128)} fusion(f32[6,128,256]{2,1,0:T(8,128)} %fusion.89, f32[1,7,128,256]{3,2,1,0:T(8,128)} %param.4), kind=kLoop, calls=%fused_computation.208 | loop fusion | flops 229376 | bytes 524288
  3.6 1.6 %bitcast_dynamic-update-slice_fusion.3 = f32[6,128,256]{2,1,0:T(8,128)} fusion(f32[6,128,256]{2,1,0:T(8,128)} %fusion.88, f32[1,7,128,256]{3,2,1,0:T(8,128)} %param.4), kind=kLoop, calls=%fused_computation.201 | loop fusion | bytes 262144
  5.2 0.8 fusion.92
  6.0 0.7 bitcast_dynamic-update-slice_fusion.1
  6.6 0.7 bitcast_dynamic-update-slice_fusion
  7.3 3.3 %collective-permute-start = (f32[6,128,256]{2,1,0:T(8,128)}, f32[6,128,256]{2,1,0:T(8,128)}, u32[]{:S(2)}, u32[]{:S(2)}) collective-permute-start(f32[6,128,256]{2,1,0:T(8,128)} %bitcast_dynamic-update-slice_fusion), channel_id=1, source_target_pairs={{0,16},{1,17},{2,18},{3,19},{4,20},{5,21},{6,22},{7,23},{8,24},{9,... | collective-permute-start | bytes 2359304 | tf_op jit(solution)/shard_map/ppermute | solution.py:27
  10.6 0.7 all_to_all.13
  11.2 7.7 %all-to-all-start.1 = ((s32[1,16,8]{2,0,1:T(1,128)}), s32[1,16,8]{2,0,1:T(1,128)S(1)}, u32[]{:S(2)}, u32[]{:S(2)}) async-start(s32[1,16,8]{2,0,1:T(1,128)} %bitcast.7), calls=%async_computation.1 | async-start | bytes 16384 | tf_op jit(solution)/shard_map/all_to_all | solution.py:167
  19.3 1.6 %fusion.83 = (f32[1,128,256]{2,1,0:T(8,128)}, f32[128,256]{1,0:T(8,128)S(1)}) fusion(f32[1,7,128,256]{3,2,1,0:T(8,128)S(1)} %copy-done, s32[128,256]{1,0:T(8,128)} %param.7, f32[128]{0:T(128)S(1)} %convert_element_type.6), kind=kLoop, calls=%fused_computation.195 | loop fusion | flops 196608 | bytes 524800 | tf_op jit(solution)/shard_map/div | solution.py:144
  21.0 0.7 copy.225
  21.7 0.8 copy.226
  22.5 0.7 copy.227
  23.6 2.6 %copy.211 = f32[6,128,256]{2,0,1:T(8,128)} copy(f32[6,128,256]{2,1,0:T(8,128)} %collective-permute-done) | data formatting | bytes 1572864 | tf_op jit(solution)/shard_map/ppermute | solution.py:27
  26.2 6.9 %all-to-all-start = ((f32[6,128,256]{2,0,1:T(8,128)}), f32[6,128,256]{2,0,1:T(8,128)S(1)}, u32[]{:S(2)}, u32[]{:S(2)}) async-start(f32[6,128,256]{2,0,1:T(8,128)} %copy.211), calls=%async_computation | async-start | bytes 2097152 | tf_op jit(solution)/shard_map/all_to_all | solution.py:166
  33.2 0.9 constant_dynamic-update-slice_fusion.6
  34.1 0.9 constant_dynamic-update-slice_fusion.5
  35.0 0.9 constant_dynamic-update-slice_fusion.4
  36.0 0.5 broadcast.439
  36.5 0.6 reduce.3
  37.2 1.0 scatter_custom_fusion
  38.2 17.4 %all-to-all-done = f32[6,128,256]{2,0,1:T(8,128)S(1)} async-done(((f32[6,128,256]{2,0,1:T(8,128)}), f32[6,128,256]{2,0,1:T(8,128)S(1)}, u32[]{:S(2)}, u32[]{:S(2)}) %all-to-all-start) | async-done | bytes 786464 | tf_op jit(solution)/shard_map/all_to_all | solution.py:166
  55.7 1.8 %gather_fusion = f32[128,6,256]{2,1,0:T(8,128)} fusion(f32[6,128,256]{2,0,1:T(8,128)S(1)} %all-to-all-done, s32[1024]{0:T(1024)S(1)} %pad_clamp_fusion.1), kind=kCustom, calls=%fused_computation | custom fusion | bytes 1573376 | tf_op jit(solution)/shard_map/gather | solution.py:171
  57.4 4.3 %fusion.122 = (f32[1,128,256]{2,0,1:T(1,128)S(1)}, f32[1,128,256]{2,0,1:T(1,128)S(1)}, f32[1,128,256]{2,0,1:T(1,128)S(1)}, f32[1,128,256]{2,0,1:T(1,128)S(1)}, f...) fusion(f32[6,128,256]{2,0,1:T(8,128)} %bitcast.344), kind=kLoop, calls=%fused_computation.251 | loop fusion | bytes 1572864 | tf_op jit(solution)/shard_map/slice | solution.py:64
  61.8 0.9 copy.216
  62.7 0.7 copy.214
  63.4 0.8 copy.221
  64.2 0.8 copy.219
  65.1 1.0 multiply_dynamic-update-slice_fusion.1
  66.2 1.0 multiply_dynamic-update-slice_fusion
  67.3 2.0 %collective-permute-start.2 = (f32[13,256,4]{1,2,0:T(4,128)S(1)}, f32[13,256,4]{1,2,0:T(4,128)S(1)}, u32[]{:S(2)}, u32[]{:S(2)}) collective-permute-start(f32[13,256,4]{1,2,0:T(4,128)S(1)} %get-tuple-element.45), channel_id=1, source_target_pairs={{1,0},{2,1},{3,2},{0,3},{5,4},{6,5},{7,6},{4,7},{9,8},{10,9},{11,1... | collective-permute-start | bytes 159752 | tf_op jit(solution)/shard_map/ppermute | solution.py:38
  69.4 0.7 copy.204
  70.2 0.8 copy.203
  70.9 0.7 copy.205
  71.7 2.7 %collective-permute-done.1 = f32[13,256,4]{1,2,0:T(4,128)S(1)} collective-permute-done((f32[13,256,4]{1,2,0:T(4,128)S(1)}, f32[13,256,4]{1,2,0:T(4,128)S(1)}, u32[]{:S(2)}, u32[]{:S(2)}) %collective-permute-start.1) | collective-permute-done | bytes 53280 | tf_op jit(solution)/shard_map/ppermute | solution.py:37
  74.4 0.6 copy-done.23
  75.4 1.1 copy.233
  76.6 1.4 %collective-permute-start.4 = (f32[13,4,136]{2,1,0:T(4,128)}, f32[13,4,136]{2,1,0:T(4,128)S(1)}, u32[]{:S(2)}, u32[]{:S(2)}) collective-permute-start(f32[13,4,136]{2,1,0:T(4,128)} %copy.233), channel_id=1, source_target_pairs={{4,0},{8,4},{12,8},{5,1},{9,5},{13,9},{6,2},{10,6},{14,10},{7,3},{... | collective-permute-start | bytes 84872 | tf_op jit(solution)/shard_map/ppermute | solution.py:38
  78.0 0.5 copy.232
  78.5 5.5 %collective-permute-start.3 = (f32[13,4,136]{2,1,0:T(4,128)S(1)}, f32[13,4,136]{2,1,0:T(4,128)}, u32[]{:S(2)}, u32[]{:S(2)}) collective-permute-start(f32[13,4,136]{2,1,0:T(4,128)S(1)} %copy.232), channel_id=1, source_target_pairs={{0,4},{4,8},{8,12},{1,5},{5,9},{9,13},{2,6},{6,10},{10,14},{3,7},{... | collective-permute-start | bytes 84872 | tf_op jit(solution)/shard_map/ppermute | solution.py:37
  84.0 1.7 %copy.242 = f32[256,128]{0,1:T(8,128)} copy(f32[256,128]{1,0:T(8,128)} %bitcast.357) | data formatting | bytes 262144 | tf_op jit(solution)/shard_map/unstack | solution.py:100
  85.6 1.7 %copy.241 = f32[256,128]{0,1:T(8,128)} copy(f32[256,128]{1,0:T(8,128)} %bitcast.355) | data formatting | bytes 262144 | tf_op jit(solution)/shard_map/unstack | solution.py:100
  87.3 1.6 %copy.239 = f32[256,128]{0,1:T(8,128)} copy(f32[256,128]{1,0:T(8,128)} %bitcast.353) | data formatting | bytes 262144 | tf_op jit(solution)/shard_map/squeeze | solution.py:63
  88.9 0.8 copy.237
  89.7 0.8 copy.251
  90.5 0.7 copy.249
  91.2 0.4 copy.235
  91.6 1.2 copy.234
  92.7 2.0 %pad_maximum_fusion = f32[13,264,136]{1,2,0:T(8,128)S(1)} fusion(f32[13,4,136]{1,2,0:T(8,128)S(1)} %copy.235, f32[13,256,4]{1,2,0:T(4,128)} %copy-done.22, f32[13,256,128]{1,2,0:T(8,128)S(1)} %constant_dynamic-update-slice_fusion, f32[13,256,4]{1,2,0:T(4,128)} %copy-done.23, f32[13,4,136]{1,2,0:T(8,128)S(1)} %copy.234), kind=kLoop, calls=%fused_computation.3 | loop fusion | flops 1867008 | bytes 3734016 | tf_op jit(solution)/shard_map/concatenate | solution.py:39
  95.6 0.8 fusion.59
  96.4 0.6 fusion.49
  97.0 0.4 add_multiply_fusion.2
  97.6 0.8 fusion.39
  98.3 0.6 fusion.29
  99.0 0.4 add_multiply_fusion.1
  99.6 0.8 fusion.19
  100.3 0.6 fusion.9
  101.0 0.4 add_multiply_fusion
  102.3 0.5 fusion.94
  103.5 0.9 gather_fusion.1
  104.4 16.7 %all_to_all.19 = f32[3,128,256]{2,0,1:T(4,128)S(1)} all-to-all(f32[3,128,256]{2,0,1:T(4,128)S(1)} %bitcast.345), channel_id=1, replica_groups=mesh['comp'=2,'lat'=4,'lon'=4] {'lat','lon'}, dimensions={1} | all-to-all | bytes 786432 | tf_op jit(solution)/shard_map/all_to_all | solution.py:186
  121.2 1.3 %collective-permute-start.5 = (f32[3,128,256]{2,1,0:T(8,128)S(1)}, f32[3,128,256]{2,1,0:T(8,128)S(1)}, u32[]{:S(2)}, u32[]{:S(2)}) collective-permute-start(f32[3,128,256]{2,1,0:T(8,128)S(1)} %copy.259), channel_id=1, source_target_pairs={{16,0},{17,1},{18,2},{19,3},{20,4},{21,5},{22,6},{23,7},{24,8},{25... | collective-permute-start | bytes 1179656 | tf_op jit(solution)/shard_map/ppermute | solution.py:27
  122.8 2.0 %collective-permute-done.5 = f32[3,128,256]{2,1,0:T(8,128)S(1)} collective-permute-done((f32[3,128,256]{2,1,0:T(8,128)S(1)}, f32[3,128,256]{2,1,0:T(8,128)S(1)}, u32[]{:S(2)}, u32[]{:S(2)}) %collective-permute-start.5) | collective-permute-done | bytes 393248 | tf_op jit(solution)/shard_map/ppermute | solution.py:27
  124.8 0.8 fusion.1
  (119 shorter events, 4.7 us)
Async XLA Ops:
  0.0 5.1 %copy-start = (f32[1,7,128,256]{3,2,1,0:T(8,128)S(1)}, f32[1,7,128,256]{3,2,1,0:T(8,128)}, u32[]{:S(2)}) copy-start(f32[1,7,128,256]{3,2,1,0:T(8,128)} %param.4) | copy-start | bytes 2752516
  0.0 10.6 %copy-start.24 = (s32[128]{0:T(128)S(1)}, s32[128]{0:T(128)}, u32[]{:S(2)}) copy-start(s32[128]{0:T(128)} %param.5) | copy-start | bytes 1540
  0.0 18.9 %copy-start.25 = (s32[128]{0:T(128)S(1)}, s32[128]{0:T(128)}, u32[]{:S(2)}) copy-start(s32[128]{0:T(128)} %param.6) | copy-start | bytes 1540
  7.3 16.3 %collective-permute-start = (f32[6,128,256]{2,1,0:T(8,128)}, f32[6,128,256]{2,1,0:T(8,128)}, u32[]{:S(2)}, u32[]{:S(2)}) collective-permute-start(f32[6,128,256]{2,1,0:T(8,128)} %bitcast_dynamic-update-slice_fusion), channel_id=1, source_target_pairs={{0,16},{1,17},{2,18},{3,19},{4,20},{5,21},{6,22},{7,23},{8,24},{9,... | collective-permute-start | bytes 2359304 | tf_op jit(solution)/shard_map/ppermute | solution.py:27
  11.2 15.0 %all-to-all-start.1 = ((s32[1,16,8]{2,0,1:T(1,128)}), s32[1,16,8]{2,0,1:T(1,128)S(1)}, u32[]{:S(2)}, u32[]{:S(2)}) async-start(s32[1,16,8]{2,0,1:T(1,128)} %bitcast.7), calls=%async_computation.1 | async-start | bytes 16384 | tf_op jit(solution)/shard_map/all_to_all | solution.py:167
  26.2 29.4 %all-to-all-start = ((f32[6,128,256]{2,0,1:T(8,128)}), f32[6,128,256]{2,0,1:T(8,128)S(1)}, u32[]{:S(2)}, u32[]{:S(2)}) async-start(f32[6,128,256]{2,0,1:T(8,128)} %copy.211), calls=%async_computation | async-start | bytes 2097152 | tf_op jit(solution)/shard_map/all_to_all | solution.py:166
  61.8 5.4 %copy-start.1 = (f32[1,128,256]{2,0,1:T(1,128)}, f32[1,128,256]{2,0,1:T(1,128)S(1)}, u32[]{:S(2)}) copy-start(f32[1,128,256]{2,0,1:T(1,128)S(1)} %get-tuple-element.46) | copy-start | bytes 393220
  61.8 5.4 %copy-start.3 = (f32[1,128,256]{2,0,1:T(1,128)}, f32[1,128,256]{2,0,1:T(1,128)S(1)}, u32[]{:S(2)}) copy-start(f32[1,128,256]{2,0,1:T(1,128)S(1)} %get-tuple-element.48) | copy-start | bytes 393220
  61.8 5.4 %copy-start.5 = (f32[1,128,256]{2,0,1:T(1,128)}, f32[1,128,256]{2,0,1:T(1,128)S(1)}, u32[]{:S(2)}) copy-start(f32[1,128,256]{2,0,1:T(1,128)S(1)} %get-tuple-element.50) | copy-start | bytes 393220
  61.8 5.4 %copy-start.9 = (f32[1,128,256]{2,0,1:T(1,128)}, f32[1,128,256]{2,0,1:T(1,128)S(1)}, u32[]{:S(2)}) copy-start(f32[1,128,256]{2,0,1:T(1,128)S(1)} %get-tuple-element.51) | copy-start | bytes 393220
  61.8 12.5 %copy-start.7 = (f32[1,128,256]{2,0,1:T(1,128)}, f32[1,128,256]{2,0,1:T(1,128)S(1)}, u32[]{:S(2)}) copy-start(f32[1,128,256]{2,0,1:T(1,128)S(1)} %get-tuple-element.49) | copy-start | bytes 393220
  61.8 12.5 %copy-start.8 = (f32[1,128,256]{2,0,1:T(1,128)}, f32[1,128,256]{2,0,1:T(1,128)S(1)}, u32[]{:S(2)}) copy-start(f32[1,128,256]{2,0,1:T(1,128)S(1)} %get-tuple-element.47) | copy-start | bytes 393220
  67.3 4.4 %collective-permute-start.2 = (f32[13,256,4]{1,2,0:T(4,128)S(1)}, f32[13,256,4]{1,2,0:T(4,128)S(1)}, u32[]{:S(2)}, u32[]{:S(2)}) collective-permute-start(f32[13,256,4]{1,2,0:T(4,128)S(1)} %get-tuple-element.45), channel_id=1, source_target_pairs={{1,0},{2,1},{3,2},{0,3},{5,4},{6,5},{7,6},{4,7},{9,8},{10,9},{11,1... | collective-permute-start | bytes 159752 | tf_op jit(solution)/shard_map/ppermute | solution.py:38
  69.3 5.0 %collective-permute-start.1 = (f32[13,256,4]{1,2,0:T(4,128)S(1)}, f32[13,256,4]{1,2,0:T(4,128)S(1)}, u32[]{:S(2)}, u32[]{:S(2)}) collective-permute-start(f32[13,256,4]{1,2,0:T(4,128)S(1)} %get-tuple-element.44), channel_id=1, source_target_pairs={{0,1},{1,2},{2,3},{3,0},{4,5},{5,6},{6,7},{7,4},{8,9},{9,10},{10,1... | collective-permute-start | bytes 159752 | tf_op jit(solution)/shard_map/ppermute | solution.py:37
  71.7 2.7 %copy-start.22 = (f32[13,256,4]{1,2,0:T(4,128)}, f32[13,256,4]{1,2,0:T(4,128)S(1)}, u32[]{:S(2)}) copy-start(f32[13,256,4]{1,2,0:T(4,128)S(1)} %collective-permute-done.2) | copy-start | bytes 159748
  74.4 0.6 copy-start.23
  76.6 12.4 %copy-start.6 = (f32[1,128,256]{2,0,1:T(1,128)S(1)}, f32[1,128,256]{2,0,1:T(1,128)}, u32[]{:S(2)}) copy-start(f32[1,128,256]{2,0,1:T(1,128)} %copy-done.5) | copy-start | bytes 393220
  76.6 13.1 %copy-start.4 = (f32[1,128,256]{2,0,1:T(1,128)S(1)}, f32[1,128,256]{2,0,1:T(1,128)}, u32[]{:S(2)}) copy-start(f32[1,128,256]{2,0,1:T(1,128)} %copy-done.3) | copy-start | bytes 393220
  76.6 13.9 %copy-start.2 = (f32[1,128,256]{2,0,1:T(1,128)S(1)}, f32[1,128,256]{2,0,1:T(1,128)}, u32[]{:S(2)}) copy-start(f32[1,128,256]{2,0,1:T(1,128)} %copy-done.1) | copy-start | bytes 393220
  76.6 14.6 %collective-permute-start.4 = (f32[13,4,136]{2,1,0:T(4,128)}, f32[13,4,136]{2,1,0:T(4,128)S(1)}, u32[]{:S(2)}, u32[]{:S(2)}) collective-permute-start(f32[13,4,136]{2,1,0:T(4,128)} %copy.233), channel_id=1, source_target_pairs={{4,0},{8,4},{12,8},{5,1},{9,5},{13,9},{6,2},{10,6},{14,10},{7,3},{... | collective-permute-start | bytes 84872 | tf_op jit(solution)/shard_map/ppermute | solution.py:38
  78.5 13.1 %collective-permute-start.3 = (f32[13,4,136]{2,1,0:T(4,128)S(1)}, f32[13,4,136]{2,1,0:T(4,128)}, u32[]{:S(2)}, u32[]{:S(2)}) collective-permute-start(f32[13,4,136]{2,1,0:T(4,128)S(1)} %copy.232), channel_id=1, source_target_pairs={{0,4},{4,8},{8,12},{1,5},{5,9},{9,13},{2,6},{6,10},{10,14},{3,7},{... | collective-permute-start | bytes 84872 | tf_op jit(solution)/shard_map/ppermute | solution.py:37
  100.9 0.9 copy-start.10
  101.0 1.0 copy-start.11
  101.0 1.0 copy-start.12
  101.0 1.1 copy-start.13
  101.0 1.1 copy-start.17
  101.0 1.2 copy-start.18
  101.0 1.2 copy-start.19
  101.0 1.2 copy-start.20
  101.0 1.3 %copy-start.21 = (f32[256,128]{0,1:T(8,128)S(1)}, f32[256,128]{0,1:T(8,128)}, u32[]{:S(2)}) copy-start(f32[256,128]{0,1:T(8,128)} %copy.249) | copy-start | bytes 393220
  102.3 0.9 copy-start.14
  104.4 20.4 %copy-start.15 = (f32[1,128,256]{2,1,0:T(8,128)S(1)}, f32[1,128,256]{2,1,0:T(8,128)}, u32[]{:S(2)}) copy-start(f32[1,128,256]{2,1,0:T(8,128)} %get-tuple-element.52) | copy-start | bytes 393220
  104.4 20.4 %copy-start.16 = (f32[1,128,256]{2,1,0:T(8,128)S(1)}, f32[1,128,256]{2,1,0:T(8,128)}, u32[]{:S(2)}) copy-start(f32[1,128,256]{2,1,0:T(8,128)} %get-tuple-element.54) | copy-start | bytes 393220
  121.2 3.6 %collective-permute-start.5 = (f32[3,128,256]{2,1,0:T(8,128)S(1)}, f32[3,128,256]{2,1,0:T(8,128)S(1)}, u32[]{:S(2)}, u32[]{:S(2)}) collective-permute-start(f32[3,128,256]{2,1,0:T(8,128)S(1)} %copy.259), channel_id=1, source_target_pairs={{16,0},{17,1},{18,2},{19,3},{20,4},{21,5},{22,6},{23,7},{24,8},{25... | collective-permute-start | bytes 1179656 | tf_op jit(solution)/shard_map/ppermute | solution.py:27
where the time goes:
time: 126 us
  local copies, waits for them, and re-layouts  39.3 us (31%)
  starting transfers between devices  28.1 us (22%)
  waiting for transfers between devices  22.1 us (18%)
  other arithmetic  18.5 us (15%)
  blocking collectives  16.7 us (13%)
    all_to_all x1, waiting for transfers between devices, per_device(): lax.all_to_all(crossed, ('lat', 'lon'), split_axis=1, concat_axis=1, tile...  17.4 us
    all_to_all x1, blocking collectives, per_device(): lax.all_to_all(back_send, ('lat', 'lon'), split_axis=1, concat_axis=1, ti...  16.7 us
    all_to_all x1, starting transfers between devices, per_device(): lax.all_to_all(owner_row, ('lat', 'lon'), split_axis=1, concat_axis=1, ti...  7.68 us
    all_to_all x1, starting transfers between devices, per_device(): lax.all_to_all(crossed, ('lat', 'lon'), split_axis=1, concat_axis=1, tile...  6.91 us
    unnamed x62, local copies, waits for them, and re-layouts  6.39 us
    unnamed x6, other arithmetic  5.66 us
    ppermute x2, starting transfers between devices, with_halo(): before = lax.ppermute(last, axis, up)  5.53 us
    ppermute x2, starting transfers between devices, from_behind(): return lax.ppermute(x, axis, pairs)  4.58 us
  transfers between devices with their start and end apart: 8, of which 3 were waited for; matrix products, arithmetic and copies ran while one was open for 18% of the time, Pallas kernels for 0%

commit v1 on v0

--- a/solution.py
+++ b/solution.py
@@ -1,6 +1,10 @@
+import functools
+
 import jax
 import jax.numpy as jnp
 from jax import lax
+from jax.experimental import pallas as pl
+from jax.experimental.pallas import tpu as pltpu
 from jax.sharding import PartitionSpec as P
 
 GX = 1
@@ -190,6 +194,441 @@
     return jnp.where(is_ocean, ocean_out, ice_out)[None]
 
 
+LEAD = 16
+TILE = 8
+MESH = pl.DeviceIdType.MESH
+DIRECTIONS = [(a, b) for a in (-1, 0, 1) for b in (-1, 0, 1) if (a, b) != (0, 0)]
+U, V, MASS, CONC, S1, S2, S12, ACTIVE, PUSH_X, PUSH_Y, CUR_X, CUR_Y = range(12)
+
+
+def split_dot(one_hot, values, contract):
+    total = None
+    rest = values
+    for piece in range(3):
+        part = rest.astype(jnp.bfloat16)
+        if piece < 2:
+            rest = rest - part.astype(jnp.float32)
+        term = lax.dot_general(
+            one_hot, part, ((contract, (0,)), ((), ())), preferred_element_type=jnp.float32
+        )
+        total = term if total is None else total + term
+    return total
+
+
+def step_kernel(
+    n_lat, n_lon,
+    fields, owner, covered, land, out,
+    surf, open_st, ret, ids, recv, grid, strength, dragb, forc, one_hot, back, land_v,
+    pack_early, pack_late, got_early, got_late,
+    load_sem, ids_ssem, ids_rsem, fwd_ssem, fwd_rsem, ret_ssem, ret_rsem,
+    early_ssem, early_rsem, late_ssem, late_rsem,
+):
+    comp = lax.axis_index("comp")
+    lat = lax.axis_index("lat")
+    lon = lax.axis_index("lon")
+    peers = n_lat * n_lon
+    me = lat * n_lon + lon
+    count = owner.shape[1]
+    per = count // peers
+    width = BX
+    barrier = pltpu.get_barrier_semaphore()
+
+    def rows_of(peer):
+        return pl.ds(pl.multiple_of(peer * per, per), per)
+
+    def device(kind, peer):
+        return (kind, peer // n_lon, peer % n_lon)
+
+    def each_peer(body):
+        def step(k, carry):
+            body((me + k) % peers)
+            return carry
+        lax.fori_loop(0, peers, step, 0)
+
+    def signal_peers(kind):
+        each_peer(
+            lambda p: pl.semaphore_signal(
+                barrier, inc=1, device_id=device(kind, p), device_id_type=MESH
+            )
+        )
+
+    def send_rows(kind, src, lo, num, dst, dlo, ssem, rsem):
+        def body(p):
+            pltpu.make_async_remote_copy(
+                src_ref=src.at[pl.ds(lo, num), rows_of(p), :],
+                dst_ref=dst.at[pl.ds(dlo, num), rows_of(me), :],
+                send_sem=ssem, recv_sem=rsem,
+                device_id=device(kind, p), device_id_type=MESH,
+            ).start()
+        each_peer(body)
+
+    def wait_bytes(ref, sem):
+        pltpu.make_async_copy(ref, ref, sem).wait()
+
+    @pl.when(comp == 0)
+    def _ocean():
+        raw = pltpu.make_async_copy(fields.at[0, pl.ds(2, 4)], surf.at[pl.ds(2, 4)], load_sem.at[0])
+        wind = pltpu.make_async_copy(fields.at[0, pl.ds(0, 2)], surf.at[pl.ds(0, 2)], load_sem.at[1])
+        rho = pltpu.make_async_copy(fields.at[0, pl.ds(6, 1)], surf.at[pl.ds(6, 1)], load_sem.at[2])
+        raw.start()
+        wind.start()
+        rho.start()
+        signal_peers(1)
+        pl.semaphore_wait(barrier, peers)
+
+        def ids_out(p):
+            pltpu.make_async_remote_copy(
+                src_ref=owner, dst_ref=ids.at[me], send_sem=ids_ssem, recv_sem=ids_rsem,
+                device_id=device(1, p), device_id_type=MESH,
+            ).start()
+        each_peer(ids_out)
+        raw.wait()
+        send_rows(1, surf, 2, 4, recv, 2, fwd_ssem.at[0], fwd_rsem.at[0])
+        wind.wait()
+        rho.wait()
+
+        def stress(t, carry):
+            r = pl.ds(pl.multiple_of(t * TILE, TILE), TILE)
+            wx, wy, density = surf[0, r, :], surf[1, r, :], surf[6, r, :]
+            scale = density * CD_ICE * jnp.sqrt(wx * wx + wy * wy + 1.0)
+            forc[0, r, :] = scale * wx
+            forc[1, r, :] = scale * wy
+            return carry
+        lax.fori_loop(0, count // TILE, stress, 0)
+        send_rows(1, forc, 0, 2, recv, 0, fwd_ssem.at[1], fwd_rsem.at[1])
+
+        def open_water(t, carry):
+            r = pl.ds(pl.multiple_of(t * TILE, TILE), TILE)
+            density = surf[6, r, :]
+            rel_x = surf[0, r, :] - surf[2, r, :]
+            rel_y = surf[1, r, :] - surf[3, r, :]
+            speed = jnp.sqrt(rel_x * rel_x + rel_y * rel_y + 1.0)
+            scale = density * (0.1 + 0.05 * speed) * speed
+            open_st[0, r, :] = scale * rel_x
+            open_st[1, r, :] = scale * rel_y
+            return carry
+        lax.fori_loop(0, count // TILE, open_water, 0)
+        wait_bytes(ret.at[pl.ds(2, 1)], ret_rsem.at[0])
+        wait_bytes(ret.at[pl.ds(0, 2)], ret_rsem.at[1])
+
+        def finish(t, carry):
+            r = pl.ds(pl.multiple_of(t * TILE, TILE), TILE)
+            water = 1.0 - ret[2, r, :]
+            out[0, 0, r, :] = ret[0, r, :] + water * open_st[0, r, :]
+            out[0, 1, r, :] = ret[1, r, :] + water * open_st[1, r, :]
+            return carry
+        lax.fori_loop(0, count // TILE, finish, 0)
+        wait_bytes(ids, ids_ssem)
+        wait_bytes(surf.at[pl.ds(2, 4)], fwd_ssem.at[0])
+        wait_bytes(forc.at[pl.ds(0, 2)], fwd_ssem.at[1])
+
+    @pl.when(comp == 1)
+    def _ice():
+        first, last = LEAD, LEAD + count
+        core = pl.ds(first, count)
+        main, side = pl.ds(0, width), pl.ds(width, width)
+        loads = [
+            pltpu.make_async_copy(
+                fields.at[0, :, :, pl.ds(y * width, width)],
+                grid.at[pl.ds(0, 7), y, core, main],
+                load_sem.at[y],
+            )
+            for y in range(2)
+        ]
+        loads.append(pltpu.make_async_copy(land, land_v, load_sem.at[2]))
+        for load in loads:
+            load.start()
+        for c in range(12):
+            for y in range(2):
+                blank = jnp.zeros((LEAD, 2 * width), jnp.float32)
+                grid[c, y, pl.ds(0, LEAD), :] = blank
+                grid[c, y, pl.ds(last, LEAD), :] = blank
+        for got in (got_early, got_late):
+            for d in range(2):
+                got[d, pl.ds(0, TILE), :] = jnp.zeros((TILE, width), jnp.float32)
+                got[d, pl.ds(TILE + count, TILE), :] = jnp.zeros((TILE, width), jnp.float32)
+
+        def inside(a):
+            if a == 0:
+                return lat >= 0
+            return lat + a >= 0 if a < 0 else lat + a < n_lat
+
+        signal_peers(0)
+        for a, b in DIRECTIONS:
+            @pl.when(inside(a))
+            def _():
+                pl.semaphore_signal(
+                    barrier, inc=1, device_id=(1, lat + a, (lon + b + n_lon) % n_lon),
+                    device_id_type=MESH,
+                )
+        walls = jnp.where(lat == 0, 3, 0) + jnp.where(lat == n_lat - 1, 3, 0)
+        pl.semaphore_wait(barrier, peers + 8 - walls)
+        for load in loads:
+            load.wait()
+
+        diag = lax.broadcasted_iota(jnp.int32, (count, count), 0) == lax.broadcasted_iota(
+            jnp.int32, (count, count), 1
+        )
+        wet = jnp.sum(
+            jnp.where(diag, covered[...].astype(jnp.float32), 0.0), axis=1, keepdims=True
+        )
+        sea = wet * (1 - land_v[...]).astype(jnp.float32)
+        for y in range(2):
+            grid[ACTIVE, y, core, main] = sea[:, y * width:(y + 1) * width]
+
+        lane = lax.broadcasted_iota(jnp.int32, (TILE, width), 1)
+
+        def pack(lo, num, packed):
+            def body(t, carry):
+                r = pl.ds(pl.multiple_of(first + t * TILE, TILE), TILE)
+                east = jnp.zeros((TILE, width), jnp.float32)
+                west = east
+                for c in range(num):
+                    for y in range(2):
+                        x = grid[lo + c, y, r, main]
+                        slot = (c * 2 + y) * NSUB
+                        mine = (lane >= slot) & (lane < slot + NSUB)
+                        east = jnp.where(mine, pltpu.roll(x, (slot + NSUB) % width, 1), east)
+                        west = jnp.where(mine, pltpu.roll(x, slot, 1) if slot else x, west)
+                q = pl.ds(pl.multiple_of(t * TILE, TILE), TILE)
+                packed[0, q, :] = east
+                packed[1, q, :] = west
+                return carry
+            lax.fori_loop(0, count // TILE, body, 0)
+
+        def halo(lo, num, packed, got, ssem, rsem, begin):
+            for k, (a, b) in enumerate(DIRECTIONS):
+                src_row = {-1: 0, 0: 0, 1: count - TILE}[a]
+                dst_row = {-1: count, 0: 0, 1: -TILE}[a]
+                rows = count if a == 0 else TILE
+                if b == 0:
+                    src = grid.at[pl.ds(lo, num), :, pl.ds(first + src_row, rows), main]
+                    dst = grid.at[pl.ds(lo, num), :, pl.ds(first + dst_row, rows), main]
+                else:
+                    d = 0 if b > 0 else 1
+                    src = packed.at[d, pl.ds(src_row, rows), :]
+                    dst = got.at[d, pl.ds(TILE + dst_row, rows), :]
+                copy = pltpu.make_async_remote_copy(
+                    src_ref=src, dst_ref=dst, send_sem=ssem.at[k], recv_sem=rsem.at[k],
+                    device_id=(1, lat + a, (lon + b + n_lon) % n_lon), device_id_type=MESH,
+                )
+                if begin:
+                    @pl.when(inside(a))
+                    def _():
+                        copy.start()
+                else:
+                    @pl.when(inside(a))
+                    def _():
+                        copy.wait_send()
+
+                    @pl.when(inside(-a))
+                    def _():
+                        copy.wait_recv()
+
+        def side_of(got, slot, q):
+            east = got[1, q, :]
+            west = got[0, q, :]
+            east = pltpu.roll(east, (width - slot) % width, 1) if slot else east
+            west = pltpu.roll(west, width - NSUB - slot, 1)
+            return jnp.where(
+                lane < NSUB, east, jnp.where(lane >= width - NSUB, west, 0.0)
+            )
+
+        def unpack(lo, num, got, after):
+            def body(t, carry):
+                q = pl.ds(pl.multiple_of(t * TILE, TILE), TILE)
+                r = pl.ds(pl.multiple_of(first + (t - 1) * TILE, TILE), TILE)
+                for c in range(num):
+                    for y in range(2):
+                        grid[lo + c, y, r, side] = side_of(got, (c * 2 + y) * NSUB, q)
+                after(r)
+                return carry
+            lax.fori_loop(0, count // TILE + 2, body, 0)
+
+        pack(0, 8, pack_early)
+        halo(0, 8, pack_early, got_early, early_ssem, early_rsem, True)
+
+        def ice_statics(r):
+            for y in range(2):
+                conc = grid[CONC, y, r, :]
+                act = grid[ACTIVE, y, r, :]
+                strength[y, r, :] = grid[MASS, y, r, :] * jnp.exp(CSTAR * (conc - 1.0)) * act
+                dragb[y, r, :] = CW * conc * act
+
+        wait_bytes(ids, ids_rsem)
+        wanted = me * per
+        row_lane = lax.broadcasted_iota(jnp.int32, (per, count), 1)
+        row_sub = lax.broadcasted_iota(jnp.int32, (per, count), 0)
+        mine = row_lane == row_sub + wanted
+        blocks = lax.broadcasted_iota(jnp.int32, (per, count), 1).astype(jnp.float32)
+        base = (me * count).astype(jnp.float32)
+        for p in range(peers):
+            owned = jnp.broadcast_to(ids[p], (per, count)).astype(jnp.float32)
+            local = jnp.sum(jnp.where(mine, owned, 0.0), axis=1, keepdims=True) - base
+            one_hot[pl.ds(p * per, per), :] = jnp.where(local == blocks, 1.0, 0.0)
+
+        halo(0, 8, pack_early, got_early, early_ssem, early_rsem, False)
+        unpack(0, 8, got_early, ice_statics)
+
+        perm = one_hot[...].astype(jnp.bfloat16)
+        wait_bytes(recv.at[pl.ds(2, 4)], fwd_rsem.at[0])
+        for c in range(2, 6):
+            forc[c] = split_dot(perm, recv[c], (0,))
+        wait_bytes(recv.at[pl.ds(0, 2)], fwd_rsem.at[1])
+        for c in range(2):
+            forc[c] = split_dot(perm, recv[c], (0,))
+
+        def pushes(t, carry):
+            q = pl.ds(pl.multiple_of(t * TILE, TILE), TILE)
+            r = pl.ds(pl.multiple_of(first + t * TILE, TILE), TILE)
+            for y in range(2):
+                half = pl.ds(y * width, width)
+                act, conc, mass = (grid[c, y, r, main] for c in (ACTIVE, CONC, MASS))
+                grid[PUSH_X, y, r, main] = act * (conc * forc[0, q, half] - mass * forc[4, q, half])
+                grid[PUSH_Y, y, r, main] = act * (conc * forc[1, q, half] - mass * forc[5, q, half])
+                grid[CUR_X, y, r, main] = forc[2, q, half]
+                grid[CUR_Y, y, r, main] = forc[3, q, half]
+            return carry
+        lax.fori_loop(0, count // TILE, pushes, 0)
+        pack(PUSH_X, 4, pack_late)
+        halo(PUSH_X, 4, pack_late, got_late, late_ssem, late_rsem, True)
+
+        for y in range(2):
+            share = grid[CONC, y, core, main] * grid[ACTIVE, y, core, main]
+            back[2, :, pl.ds(y * width, width)] = split_dot(perm, share, (1,))
+        send_rows(0, back, 2, 1, ret, 2, ret_ssem.at[0], ret_rsem.at[0])
+
+        halo(PUSH_X, 4, pack_late, got_late, late_ssem, late_rsem, False)
+        unpack(PUSH_X, 4, got_late, lambda r: None)
+
+        def east_of(x):
+            return pltpu.roll(x, 2 * width - 1, 1)
+
+        def west_of(x):
+            return pltpu.roll(x, 1, 1)
+
+        sub = lax.broadcasted_iota(jnp.int32, (TILE, 2 * width), 0)
+
+        def next_row(x, after):
+            return pltpu.roll(jnp.where(sub == 0, after, x), TILE - 1, 0)
+
+        def last_row(x, before):
+            return pltpu.roll(jnp.where(sub == TILE - 1, before, x), 1, 0)
+
+        def sweep(t):
+            base_row = pl.multiple_of(first - TILE + t * TILE, TILE)
+            r = pl.ds(base_row, TILE)
+            nxt = pl.ds(pl.multiple_of(base_row + TILE, TILE), TILE)
+            prev = pl.ds(pl.multiple_of(base_row - TILE, TILE), TILE)
+            u = [grid[U, 0, r, :], grid[U, 1, r, :]]
+            v = [grid[V, 0, r, :], grid[V, 1, r, :]]
+            u_up = [u[1], next_row(u[0], grid[U, 0, nxt, :])]
+            v_up = [v[1], next_row(v[0], grid[V, 0, nxt, :])]
+            diag_xx, diag_yy, cross = [], [], []
+            for y in range(2):
+                sxx = east_of(u[y]) - u[y]
+                syy = v_up[y] - v[y]
+                shear = (u_up[y] - u[y]) + (east_of(v[y]) - v[y])
+                div = sxx + syy
+                ten = sxx - syy
+                delta = jnp.sqrt(div * div + (ten * ten + shear * shear) * (1.0 / ECC2) + DMIN2)
+                visc = RELAX * strength[y, r, :] / delta
+                scale = 1.0 / (1.0 + RELAX)
+                s1 = (grid[S1, y, r, :] + visc * (div - delta)) * scale
+                s2 = (grid[S2, y, r, :] + visc * ten * (1.0 / ECC2)) * scale
+                s12 = (grid[S12, y, r, :] + visc * shear * (0.5 / ECC2)) * scale
+                grid[S1, y, r, :] = s1
+                grid[S2, y, r, :] = s2
+                grid[S12, y, r, :] = s12
+                diag_xx.append(0.5 * (s1 + s2))
+                diag_yy.append(0.5 * (s1 - s2))
+                cross.append(s12)
+            yy_before = 0.5 * (grid[S1, 1, prev, :] - grid[S2, 1, prev, :])
+            yy_down = [last_row(diag_yy[1], yy_before), diag_yy[0]]
+            cross_down = [last_row(cross[1], grid[S12, 1, prev, :]), cross[0]]
+            for y in range(2):
+                force_x = diag_xx[y] - west_of(diag_xx[y]) + (cross[y] - cross_down[y])
+                force_y = cross[y] - west_of(cross[y]) + (diag_yy[y] - yy_down[y])
+                mass = grid[MASS, y, r, :]
+                act = grid[ACTIVE, y, r, :]
+                cx, cy = grid[CUR_X, y, r, :], grid[CUR_Y, y, r, :]
+                dx, dy = cx - u[y], cy - v[y]
+                drag = dragb[y, r, :] * jnp.sqrt(dx * dx + dy * dy + DRAG_FLOOR)
+                gain = act / (jnp.maximum(mass, MASS_FLOOR) * (1.0 / DTE) + drag)
+                inertia = mass * (1.0 / DTE)
+                turn = CORIO * mass
+                grid[U, y, r, :] = gain * (
+                    inertia * u[y] + force_x + grid[PUSH_X, y, r, :] + drag * cx + turn * v[y]
+                )
+                grid[V, y, r, :] = gain * (
+                    inertia * v[y] + force_y + grid[PUSH_Y, y, r, :] + drag * cy - turn * u[y]
+                )
+
+        def sweeps(k, carry):
+            sweep(k % (count // TILE + 2))
+            return carry
+        lax.fori_loop(0, NSUB * (count // TILE + 2), sweeps, 0)
+
+        def returned(t, carry):
+            q = pl.ds(pl.multiple_of(t * TILE, TILE), TILE)
+            r = pl.ds(pl.multiple_of(first + t * TILE, TILE), TILE)
+            for y in range(2):
+                half = pl.ds(y * width, width)
+                u, v = grid[U, y, r, main], grid[V, y, r, main]
+                out[0, 0, q, half] = u
+                out[0, 1, q, half] = v
+                dx, dy = u - grid[CUR_X, y, r, main], v - grid[CUR_Y, y, r, main]
+                drag = dragb[y, r, main] * jnp.sqrt(dx * dx + dy * dy + DRAG_FLOOR)
+                forc[0, q, half] = drag * dx
+                forc[1, q, half] = drag * dy
+            return carry
+        lax.fori_loop(0, count // TILE, returned, 0)
+        for c in range(2):
+            back[c] = split_dot(perm, forc[c], (1,))
+        send_rows(0, back, 0, 2, ret, 0, ret_ssem.at[1], ret_rsem.at[1])
+        wait_bytes(back.at[pl.ds(2, 1)], ret_ssem.at[0])
+        wait_bytes(back.at[pl.ds(0, 2)], ret_ssem.at[1])
+
+
+def per_device_kernel(n_lat, n_lon, fields, block_owner, ice_covered, land_mask):
+    count, cells = land_mask.shape
+    peers = n_lat * n_lon
+    long = count + 2 * LEAD
+    f32 = jnp.float32
+    anywhere = pl.BlockSpec(memory_space=pl.ANY)
+    in_vmem = pl.BlockSpec(memory_space=pltpu.VMEM)
+    dma = pltpu.SemaphoreType.DMA
+    return pl.pallas_call(
+        functools.partial(step_kernel, n_lat, n_lon),
+        out_shape=jax.ShapeDtypeStruct((1, 2, count, cells), f32),
+        in_specs=[anywhere, in_vmem, in_vmem, anywhere],
+        out_specs=in_vmem,
+        scratch_shapes=[
+            pltpu.VMEM((7, count, cells), f32),
+            pltpu.VMEM((2, count, cells), f32),
+            pltpu.VMEM((3, count, cells), f32),
+            pltpu.VMEM((peers, 1, count), jnp.int32),
+            pltpu.VMEM((6, count, cells), f32),
+            pltpu.VMEM((12, 2, long, 2 * BX), f32),
+            pltpu.VMEM((2, long, 2 * BX), f32),
+            pltpu.VMEM((2, long, 2 * BX), f32),
+            pltpu.VMEM((6, count, cells), f32),
+            pltpu.VMEM((count, count), f32),
+            pltpu.VMEM((3, count, cells), f32),
+            pltpu.VMEM((count, cells), jnp.int32),
+            pltpu.VMEM((2, count, BX), f32),
+            pltpu.VMEM((2, count, BX), f32),
+            pltpu.VMEM((2, count + 2 * TILE, BX), f32),
+            pltpu.VMEM((2, count + 2 * TILE, BX), f32),
+            dma((3,)), dma, dma, dma((2,)), dma((2,)), dma((2,)), dma((2,)),
+            dma((8,)), dma((8,)), dma((8,)), dma((8,)),
+        ],
+        compiler_params=pltpu.CompilerParams(
+            collective_id=0, has_side_effects=True, vmem_limit_bytes=40 * 1024 * 1024
+        ),
+    )(fields, block_owner.reshape(1, count), ice_covered.reshape(1, count), land_mask)
+
+
 def solution(mesh):
     placed = (
         P("comp", None, ("lat", "lon"), None),
@@ -197,8 +636,17 @@
         P(("lat", "lon")),
         P(("lat", "lon"), None),
     )
+    n_lat, n_lon = mesh.shape["lat"], mesh.shape["lon"]
+
+    def body(fields, block_owner, ice_covered, land_mask):
+        count = block_owner.shape[0]
+        whole_tiles = count % (n_lat * n_lon * TILE) == 0 and count == BX
+        if whole_tiles and n_lon > 2:
+            return per_device_kernel(n_lat, n_lon, fields, block_owner, ice_covered, land_mask)
+        return per_device(fields, block_owner, ice_covered, land_mask)
+
     return jax.shard_map(
-        per_device,
+        body,
         mesh=mesh,
         in_specs=placed,
         out_specs=P("comp", None, ("lat", "lon"), None),

time: 126 us -> 48.5 us (0.38)
  Pallas kernels: 0 us -> 44.8 us
  local copies, waits for them, and re-layouts: 39.3 us -> 3.46 us
  starting transfers between devices: 28.1 us -> 0 us
  waiting for transfers between devices: 22.1 us -> 0 us
  other arithmetic: 18.5 us -> 0 us
  blocking collectives: 16.7 us -> 0 us
    pallas_call x0 -> x1, Pallas kernels: none -> 44.8 us  [per_device_kernel(): pl.pallas_call(functools.partial(step_kernel, n_lat, n_lon), out_shape=ja...]
    all_to_all x2 -> x0, waiting for transfers between devices: 17.4 us -> none  [the longest x1 17.4 us: per_device(): lax.all_to_all(crossed, ('lat', 'lon'), split_axis=1, concat_axis=1, tile...]
    all_to_all x1 -> x0, blocking collectives: 16.7 us -> none  [per_device(): lax.all_to_all(back_send, ('lat', 'lon'), split_axis=1, concat_axis=1, ti...]
    all_to_all x2 -> x0, starting transfers between devices: 14.6 us -> none  [the longest x1 7.68 us: per_device(): lax.all_to_all(owner_row, ('lat', 'lon'), split_axis=1, concat_axis=1, ti...]
    ppermute x6 -> x0, starting transfers between devices: 13.5 us -> none  [the longest x2 5.53 us: with_halo(): before = lax.ppermute(last, axis, up)]
    slice x18 -> x0, local copies, waits for them, and re-layouts: 9.03 us -> none  [the longest x1 4.34 us: prepare(): push_y = active * (concentration * forcing[1] - ice_mass * forcing[5])]
    squeeze x18 -> x0, local copies, waits for them, and re-layouts: 8.42 us -> none  [the longest x4 3.99 us: prepare(): push_x = active * (concentration * forcing[0] - ice_mass * forcing[4])]
    div x11 -> x0, other arithmetic: 6.28 us -> none  [the longest x3 2.27 us: subcycle(): active * (ice_mass / DTE * east_old + force_x + push_x + drag_coef * curr...]
  transfers between devices with their start and end apart: 8 -> 0, of which waited for: 3 -> 0; matrix products, arithmetic and copies ran while one was open for 18% -> 0% of each run, Pallas kernels for 0% -> 0%
where the time goes in v1:
time: 48.5 us; the launch traced here: 48.3 us
  Pallas kernels  44.8 us (92%)
  local copies, waits for them, and re-layouts  3.46 us (7%)
    pallas_call x1, Pallas kernels, per_device_kernel(): pl.pallas_call(functools.partial(step_kernel, n_lat, n_lon), out_shape=ja...  44.8 us
    unnamed x9, local copies, waits for them, and re-layouts  3.46 us

profile of v1, /device:TPU:0, one launch (start us, length us, event | category | flops | bytes accessed | tf_op | source)
XLA Modules:
  0.0 48.3 jit_solution(16804269777473142753)
XLA Ops:
  0.0 0.0 copy-start.2
  0.0 0.0 copy-start.3
  0.0 0.7 %copy-done.2 = s32[128]{0:T(128)S(1)} copy-done((s32[128]{0:T(128)S(1)}, s32[128]{0:T(128)}, u32[]{:S(2)}) %copy-start.2) | copy-done | bytes 536
  0.7 0.0 copy-done.3
  0.7 0.0 copy-start
  0.7 1.2 %copy-done = f32[1,7,128,256]{3,2,1,0:T(8,128)S(1)} copy-done((f32[1,7,128,256]{3,2,1,0:T(8,128)S(1)}, f32[1,7,128,256]{3,2,1,0:T(8,128)}, u32[]{:S(2)}) %copy-start) | copy-done | bytes 917528
  1.9 0.0 copy-start.1
  1.9 0.9 %copy-done.1 = s32[128,256]{1,0:T(8,128)S(1)} copy-done((s32[128,256]{1,0:T(8,128)S(1)}, s32[128,256]{1,0:T(8,128)}, u32[]{:S(2)}) %copy-start.1) | copy-done | bytes 131096
  2.8 44.8 %shard_map.46 = f32[1,2,128,256]{3,2,1,0:T(8,128)S(1)} custom-call(f32[1,7,128,256]{3,2,1,0:T(8,128)S(1)} %copy-done, s32[1,128]{1,0:T(1,128)S(1)} %bitcast.2, s32[1,128]{1,0:T(1,128)S(1)} %bitcast.3, s32[128,256]{1,0:T(8,128)S(1)} %copy-done.1), custom_call_target="tpu_custom_call" | custom-call | tf_op jit(solution)/shard_map/pallas_call | solution.py:601
  47.6 0.7 %copy.6 = f32[1,2,128,256]{3,2,1,0:T(8,128)} copy(f32[1,2,128,256]{3,2,1,0:T(8,128)S(1)} %shard_map.46) | data formatting | bytes 524288
Async XLA Ops:
  0.0 0.7 %copy-start.2 = (s32[128]{0:T(128)S(1)}, s32[128]{0:T(128)}, u32[]{:S(2)}) copy-start(s32[128]{0:T(128)} %param.5) | copy-start | bytes 1540
  0.0 0.7 %copy-start.3 = (s32[128]{0:T(128)S(1)}, s32[128]{0:T(128)}, u32[]{:S(2)}) copy-start(s32[128]{0:T(128)} %param.6) | copy-start | bytes 1540
  0.7 1.2 %copy-start = (f32[1,7,128,256]{3,2,1,0:T(8,128)S(1)}, f32[1,7,128,256]{3,2,1,0:T(8,128)}, u32[]{:S(2)}) copy-start(f32[1,7,128,256]{3,2,1,0:T(8,128)} %fields.1) | copy-start | bytes 2752516
  1.9 0.9 %copy-start.1 = (s32[128,256]{1,0:T(8,128)S(1)}, s32[128,256]{1,0:T(8,128)}, u32[]{:S(2)}) copy-start(s32[128,256]{1,0:T(8,128)} %land.1) | copy-start | bytes 393220

commit v2 on v1

--- a/solution.py
+++ b/solution.py
@@ -195,10 +195,19 @@
 
 
 LEAD = 16
+GROUP = 3
 TILE = 8
 MESH = pl.DeviceIdType.MESH
 DIRECTIONS = [(a, b) for a in (-1, 0, 1) for b in (-1, 0, 1) if (a, b) != (0, 0)]
 U, V, MASS, CONC, S1, S2, S12, ACTIVE, PUSH_X, PUSH_Y, CUR_X, CUR_Y = range(12)
+
+
+def tile_loop(tiles, together, body):
+    def step(k, carry):
+        for j in range(together):
+            body(k * together + j)
+        return carry
+    lax.fori_loop(0, tiles // together, step, 0)
 
 
 def split_dot(one_hot, values, contract):
@@ -219,9 +228,9 @@
     n_lat, n_lon,
     fields, owner, covered, land, out,
     surf, open_st, ret, ids, recv, grid, strength, dragb, forc, one_hot, back, land_v,
-    pack_early, pack_late, got_early, got_late,
+    pack_early, pack_mid, pack_late, got_early, got_mid, got_late,
     load_sem, ids_ssem, ids_rsem, fwd_ssem, fwd_rsem, ret_ssem, ret_rsem,
-    early_ssem, early_rsem, late_ssem, late_rsem,
+    early_ssem, early_rsem, mid_ssem, mid_rsem, late_ssem, late_rsem,
 ):
     comp = lax.axis_index("comp")
     lat = lax.axis_index("lat")
@@ -241,7 +250,7 @@
 
     def each_peer(body):
         def step(k, carry):
-            body((me + k) % peers)
+            body((me + peers // 2 + k) % peers)
             return carry
         lax.fori_loop(0, peers, step, 0)
 
@@ -287,17 +296,17 @@
         wind.wait()
         rho.wait()
 
-        def stress(t, carry):
+        def stress(t):
             r = pl.ds(pl.multiple_of(t * TILE, TILE), TILE)
             wx, wy, density = surf[0, r, :], surf[1, r, :], surf[6, r, :]
             scale = density * CD_ICE * jnp.sqrt(wx * wx + wy * wy + 1.0)
             forc[0, r, :] = scale * wx
             forc[1, r, :] = scale * wy
-            return carry
-        lax.fori_loop(0, count // TILE, stress, 0)
+
+        tile_loop(count // TILE, 2, stress)
         send_rows(1, forc, 0, 2, recv, 0, fwd_ssem.at[1], fwd_rsem.at[1])
 
-        def open_water(t, carry):
+        def open_water(t):
             r = pl.ds(pl.multiple_of(t * TILE, TILE), TILE)
             density = surf[6, r, :]
             rel_x = surf[0, r, :] - surf[2, r, :]
@@ -306,18 +315,18 @@
             scale = density * (0.1 + 0.05 * speed) * speed
             open_st[0, r, :] = scale * rel_x
             open_st[1, r, :] = scale * rel_y
-            return carry
-        lax.fori_loop(0, count // TILE, open_water, 0)
+
+        tile_loop(count // TILE, 2, open_water)
         wait_bytes(ret.at[pl.ds(2, 1)], ret_rsem.at[0])
         wait_bytes(ret.at[pl.ds(0, 2)], ret_rsem.at[1])
 
-        def finish(t, carry):
+        def finish(t):
             r = pl.ds(pl.multiple_of(t * TILE, TILE), TILE)
             water = 1.0 - ret[2, r, :]
             out[0, 0, r, :] = ret[0, r, :] + water * open_st[0, r, :]
             out[0, 1, r, :] = ret[1, r, :] + water * open_st[1, r, :]
-            return carry
-        lax.fori_loop(0, count // TILE, finish, 0)
+
+        tile_loop(count // TILE, 2, finish)
         wait_bytes(ids, ids_ssem)
         wait_bytes(surf.at[pl.ds(2, 4)], fwd_ssem.at[0])
         wait_bytes(forc.at[pl.ds(0, 2)], fwd_ssem.at[1])
@@ -343,7 +352,7 @@
                 blank = jnp.zeros((LEAD, 2 * width), jnp.float32)
                 grid[c, y, pl.ds(0, LEAD), :] = blank
                 grid[c, y, pl.ds(last, LEAD), :] = blank
-        for got in (got_early, got_late):
+        for got in (got_early, got_mid, got_late):
             for d in range(2):
                 got[d, pl.ds(0, TILE), :] = jnp.zeros((TILE, width), jnp.float32)
                 got[d, pl.ds(TILE + count, TILE), :] = jnp.zeros((TILE, width), jnp.float32)
@@ -379,7 +388,7 @@
         lane = lax.broadcasted_iota(jnp.int32, (TILE, width), 1)
 
         def pack(lo, num, packed):
-            def body(t, carry):
+            def body(t):
                 r = pl.ds(pl.multiple_of(first + t * TILE, TILE), TILE)
                 east = jnp.zeros((TILE, width), jnp.float32)
                 west = east
@@ -393,8 +402,7 @@
                 q = pl.ds(pl.multiple_of(t * TILE, TILE), TILE)
                 packed[0, q, :] = east
                 packed[1, q, :] = west
-                return carry
-            lax.fori_loop(0, count // TILE, body, 0)
+            tile_loop(count // TILE, 2, body)
 
         def halo(lo, num, packed, got, ssem, rsem, begin):
             for k, (a, b) in enumerate(DIRECTIONS):
@@ -435,15 +443,14 @@
             )
 
         def unpack(lo, num, got, after):
-            def body(t, carry):
+            def body(t):
                 q = pl.ds(pl.multiple_of(t * TILE, TILE), TILE)
                 r = pl.ds(pl.multiple_of(first + (t - 1) * TILE, TILE), TILE)
                 for c in range(num):
                     for y in range(2):
                         grid[lo + c, y, r, side] = side_of(got, (c * 2 + y) * NSUB, q)
                 after(r)
-                return carry
-            lax.fori_loop(0, count // TILE + 2, body, 0)
+            tile_loop(count // TILE + 2, 2, body)
 
         pack(0, 8, pack_early)
         halo(0, 8, pack_early, got_early, early_ssem, early_rsem, True)
@@ -452,7 +459,9 @@
             for y in range(2):
                 conc = grid[CONC, y, r, :]
                 act = grid[ACTIVE, y, r, :]
-                strength[y, r, :] = grid[MASS, y, r, :] * jnp.exp(CSTAR * (conc - 1.0)) * act
+                strength[y, r, :] = (
+                    (RELAX / (1.0 + RELAX)) * grid[MASS, y, r, :] * jnp.exp(CSTAR * (conc - 1.0)) * act
+                )
                 dragb[y, r, :] = CW * conc * act
 
         wait_bytes(ids, ids_rsem)
@@ -470,106 +479,138 @@
         halo(0, 8, pack_early, got_early, early_ssem, early_rsem, False)
         unpack(0, 8, got_early, ice_statics)
 
+        def east_of(x):
+            return pltpu.roll(x, 2 * width - 1, 1)
+
+        def west_of(x):
+            return pltpu.roll(x, 1, 1)
+
+        sub = lax.broadcasted_iota(jnp.int32, (TILE, 2 * width), 0)
+
+        def next_row(x, after):
+            return pltpu.roll(jnp.where(sub == 0, after, x), TILE - 1, 0)
+
+        def last_row(x, before):
+            return pltpu.roll(jnp.where(sub == TILE - 1, before, x), 1, 0)
+
+        def sweep(g, new_stress, new_velocity):
+            spots = [
+                pl.ds(pl.multiple_of(first + (g * GROUP + j - 2) * TILE, TILE), TILE)
+                for j in range(GROUP + 2)
+            ]
+            before, spots, after = spots[0], spots[1:-1], spots[-1]
+            keep = 1.0 / (1.0 + RELAX)
+            vels, stresses = [], []
+            for r in spots:
+                vels.append([(grid[U, y, r, :], grid[V, y, r, :]) for y in range(2)])
+            if new_stress:
+                follow = (grid[U, 0, after, :], grid[V, 0, after, :])
+            for j, r in enumerate(spots):
+                if not new_stress:
+                    stresses.append(
+                        [tuple(grid[c, y, r, :] for c in (S1, S2, S12)) for y in range(2)]
+                    )
+                    continue
+                beyond = vels[j + 1][0] if j + 1 < GROUP else follow
+                row = []
+                for y in range(2):
+                    u, v = vels[j][y]
+                    if y == 0:
+                        u_up, v_up = vels[j][1]
+                    else:
+                        u_up = next_row(vels[j][0][0], beyond[0])
+                        v_up = next_row(vels[j][0][1], beyond[1])
+                    sxx = east_of(u) - u
+                    syy = v_up - v
+                    shear = (u_up - u) + (east_of(v) - v)
+                    div = sxx + syy
+                    ten = sxx - syy
+                    square = div * div + (ten * ten + shear * shear) * (1.0 / ECC2) + DMIN2
+                    inverse = lax.rsqrt(square)
+                    visc = strength[y, r, :] * inverse
+                    s1 = grid[S1, y, r, :] * keep + visc * (div - square * inverse)
+                    s2 = grid[S2, y, r, :] * keep + visc * ten * (1.0 / ECC2)
+                    s12 = grid[S12, y, r, :] * keep + visc * shear * (0.5 / ECC2)
+                    grid[S1, y, r, :] = s1
+                    grid[S2, y, r, :] = s2
+                    grid[S12, y, r, :] = s12
+                    row.append((s1, s2, s12))
+                stresses.append(row)
+            if not new_velocity:
+                return
+            yy_before = 0.5 * (grid[S1, 1, before, :] - grid[S2, 1, before, :])
+            cross_before = grid[S12, 1, before, :]
+            for j, r in enumerate(spots):
+                xx = [0.5 * (s1 + s2) for s1, s2, _ in stresses[j]]
+                yy = [0.5 * (s1 - s2) for s1, s2, _ in stresses[j]]
+                cross = [s12 for _, _, s12 in stresses[j]]
+                yy_down = [last_row(yy[1], yy_before), yy[0]]
+                cross_down = [last_row(cross[1], cross_before), cross[0]]
+                yy_before, cross_before = yy[1], cross[1]
+                for y in range(2):
+                    u, v = vels[j][y]
+                    force_x = xx[y] - west_of(xx[y]) + (cross[y] - cross_down[y])
+                    force_y = cross[y] - west_of(cross[y]) + (yy[y] - yy_down[y])
+                    mass = grid[MASS, y, r, :]
+                    cx, cy = grid[CUR_X, y, r, :], grid[CUR_Y, y, r, :]
+                    dx, dy = cx - u, cy - v
+                    square = dx * dx + dy * dy + DRAG_FLOOR
+                    drag = dragb[y, r, :] * (square * lax.rsqrt(square))
+                    gain = grid[ACTIVE, y, r, :] / (
+                        jnp.maximum(mass, MASS_FLOOR) * (1.0 / DTE) + drag
+                    )
+                    inertia = mass * (1.0 / DTE)
+                    turn = CORIO * mass
+                    grid[U, y, r, :] = gain * (
+                        inertia * u + force_x + grid[PUSH_X, y, r, :] + drag * cx + turn * v
+                    )
+                    grid[V, y, r, :] = gain * (
+                        inertia * v + force_y + grid[PUSH_Y, y, r, :] + drag * cy - turn * u
+                    )
+
+        groups = (count // TILE + 2) // GROUP
+
+        def stress_only():
+            tile_loop(groups, 1, lambda g: sweep(g, True, False))
+
         perm = one_hot[...].astype(jnp.bfloat16)
+        stress_only()
         wait_bytes(recv.at[pl.ds(2, 4)], fwd_rsem.at[0])
-        for c in range(2, 6):
-            forc[c] = split_dot(perm, recv[c], (0,))
+        for c in range(2):
+            both = split_dot(perm, recv[2 + c], (0,))
+            for y in range(2):
+                grid[CUR_X + c, y, core, main] = both[:, y * width:(y + 1) * width]
+        pack(CUR_X, 2, pack_mid)
+        halo(CUR_X, 2, pack_mid, got_mid, mid_ssem, mid_rsem, True)
+        for c in range(2):
+            both = split_dot(perm, recv[4 + c], (0,))
+            for y in range(2):
+                part = both[:, y * width:(y + 1) * width]
+                grid[PUSH_X + c, y, core, main] = grid[MASS, y, core, main] * part
+        halo(CUR_X, 2, pack_mid, got_mid, mid_ssem, mid_rsem, False)
+        unpack(CUR_X, 2, got_mid, lambda r: None)
         wait_bytes(recv.at[pl.ds(0, 2)], fwd_rsem.at[1])
         for c in range(2):
-            forc[c] = split_dot(perm, recv[c], (0,))
-
-        def pushes(t, carry):
-            q = pl.ds(pl.multiple_of(t * TILE, TILE), TILE)
-            r = pl.ds(pl.multiple_of(first + t * TILE, TILE), TILE)
+            both = split_dot(perm, recv[c], (0,))
             for y in range(2):
-                half = pl.ds(y * width, width)
-                act, conc, mass = (grid[c, y, r, main] for c in (ACTIVE, CONC, MASS))
-                grid[PUSH_X, y, r, main] = act * (conc * forc[0, q, half] - mass * forc[4, q, half])
-                grid[PUSH_Y, y, r, main] = act * (conc * forc[1, q, half] - mass * forc[5, q, half])
-                grid[CUR_X, y, r, main] = forc[2, q, half]
-                grid[CUR_Y, y, r, main] = forc[3, q, half]
-            return carry
-        lax.fori_loop(0, count // TILE, pushes, 0)
-        pack(PUSH_X, 4, pack_late)
-        halo(PUSH_X, 4, pack_late, got_late, late_ssem, late_rsem, True)
+                part = both[:, y * width:(y + 1) * width]
+                grid[PUSH_X + c, y, core, main] = grid[ACTIVE, y, core, main] * (
+                    grid[CONC, y, core, main] * part - grid[PUSH_X + c, y, core, main]
+                )
+        pack(PUSH_X, 2, pack_late)
+        halo(PUSH_X, 2, pack_late, got_late, late_ssem, late_rsem, True)
 
         for y in range(2):
             share = grid[CONC, y, core, main] * grid[ACTIVE, y, core, main]
             back[2, :, pl.ds(y * width, width)] = split_dot(perm, share, (1,))
         send_rows(0, back, 2, 1, ret, 2, ret_ssem.at[0], ret_rsem.at[0])
 
-        halo(PUSH_X, 4, pack_late, got_late, late_ssem, late_rsem, False)
-        unpack(PUSH_X, 4, got_late, lambda r: None)
-
-        def east_of(x):
-            return pltpu.roll(x, 2 * width - 1, 1)
-
-        def west_of(x):
-            return pltpu.roll(x, 1, 1)
-
-        sub = lax.broadcasted_iota(jnp.int32, (TILE, 2 * width), 0)
-
-        def next_row(x, after):
-            return pltpu.roll(jnp.where(sub == 0, after, x), TILE - 1, 0)
-
-        def last_row(x, before):
-            return pltpu.roll(jnp.where(sub == TILE - 1, before, x), 1, 0)
-
-        def sweep(t):
-            base_row = pl.multiple_of(first - TILE + t * TILE, TILE)
-            r = pl.ds(base_row, TILE)
-            nxt = pl.ds(pl.multiple_of(base_row + TILE, TILE), TILE)
-            prev = pl.ds(pl.multiple_of(base_row - TILE, TILE), TILE)
-            u = [grid[U, 0, r, :], grid[U, 1, r, :]]
-            v = [grid[V, 0, r, :], grid[V, 1, r, :]]
-            u_up = [u[1], next_row(u[0], grid[U, 0, nxt, :])]
-            v_up = [v[1], next_row(v[0], grid[V, 0, nxt, :])]
-            diag_xx, diag_yy, cross = [], [], []
-            for y in range(2):
-                sxx = east_of(u[y]) - u[y]
-                syy = v_up[y] - v[y]
-                shear = (u_up[y] - u[y]) + (east_of(v[y]) - v[y])
-                div = sxx + syy
-                ten = sxx - syy
-                delta = jnp.sqrt(div * div + (ten * ten + shear * shear) * (1.0 / ECC2) + DMIN2)
-                visc = RELAX * strength[y, r, :] / delta
-                scale = 1.0 / (1.0 + RELAX)
-                s1 = (grid[S1, y, r, :] + visc * (div - delta)) * scale
-                s2 = (grid[S2, y, r, :] + visc * ten * (1.0 / ECC2)) * scale
-                s12 = (grid[S12, y, r, :] + visc * shear * (0.5 / ECC2)) * scale
-                grid[S1, y, r, :] = s1
-                grid[S2, y, r, :] = s2
-                grid[S12, y, r, :] = s12
-                diag_xx.append(0.5 * (s1 + s2))
-                diag_yy.append(0.5 * (s1 - s2))
-                cross.append(s12)
-            yy_before = 0.5 * (grid[S1, 1, prev, :] - grid[S2, 1, prev, :])
-            yy_down = [last_row(diag_yy[1], yy_before), diag_yy[0]]
-            cross_down = [last_row(cross[1], grid[S12, 1, prev, :]), cross[0]]
-            for y in range(2):
-                force_x = diag_xx[y] - west_of(diag_xx[y]) + (cross[y] - cross_down[y])
-                force_y = cross[y] - west_of(cross[y]) + (diag_yy[y] - yy_down[y])
-                mass = grid[MASS, y, r, :]
-                act = grid[ACTIVE, y, r, :]
-                cx, cy = grid[CUR_X, y, r, :], grid[CUR_Y, y, r, :]
-                dx, dy = cx - u[y], cy - v[y]
-                drag = dragb[y, r, :] * jnp.sqrt(dx * dx + dy * dy + DRAG_FLOOR)
-                gain = act / (jnp.maximum(mass, MASS_FLOOR) * (1.0 / DTE) + drag)
-                inertia = mass * (1.0 / DTE)
-                turn = CORIO * mass
-                grid[U, y, r, :] = gain * (
-                    inertia * u[y] + force_x + grid[PUSH_X, y, r, :] + drag * cx + turn * v[y]
-                )
-                grid[V, y, r, :] = gain * (
-                    inertia * v[y] + force_y + grid[PUSH_Y, y, r, :] + drag * cy - turn * u[y]
-                )
-
-        def sweeps(k, carry):
-            sweep(k % (count // TILE + 2))
-            return carry
-        lax.fori_loop(0, NSUB * (count // TILE + 2), sweeps, 0)
-
-        def returned(t, carry):
+        halo(PUSH_X, 2, pack_late, got_late, late_ssem, late_rsem, False)
+        unpack(PUSH_X, 2, got_late, lambda r: None)
+        tile_loop(groups, 1, lambda g: sweep(g, False, True))
+        tile_loop((NSUB - 1) * groups, 1, lambda k: sweep(k % groups, True, True))
+
+        def returned(t):
             q = pl.ds(pl.multiple_of(t * TILE, TILE), TILE)
             r = pl.ds(pl.multiple_of(first + t * TILE, TILE), TILE)
             for y in range(2):
@@ -581,8 +622,8 @@
                 drag = dragb[y, r, main] * jnp.sqrt(dx * dx + dy * dy + DRAG_FLOOR)
                 forc[0, q, half] = drag * dx
                 forc[1, q, half] = drag * dy
-            return carry
-        lax.fori_loop(0, count // TILE, returned, 0)
+
+        tile_loop(count // TILE, 2, returned)
         for c in range(2):
             back[c] = split_dot(perm, forc[c], (1,))
         send_rows(0, back, 0, 2, ret, 0, ret_ssem.at[1], ret_rsem.at[1])
@@ -618,13 +659,15 @@
             pltpu.VMEM((count, cells), jnp.int32),
             pltpu.VMEM((2, count, BX), f32),
             pltpu.VMEM((2, count, BX), f32),
+            pltpu.VMEM((2, count, BX), f32),
+            pltpu.VMEM((2, count + 2 * TILE, BX), f32),
             pltpu.VMEM((2, count + 2 * TILE, BX), f32),
             pltpu.VMEM((2, count + 2 * TILE, BX), f32),
             dma((3,)), dma, dma, dma((2,)), dma((2,)), dma((2,)), dma((2,)),
-            dma((8,)), dma((8,)), dma((8,)), dma((8,)),
+            dma((8,)), dma((8,)), dma((8,)), dma((8,)), dma((8,)), dma((8,)),
         ],
         compiler_params=pltpu.CompilerParams(
-            collective_id=0, has_side_effects=True, vmem_limit_bytes=40 * 1024 * 1024
+            collective_id=0, has_side_effects=True, vmem_limit_bytes=63 * 1024 * 1024
         ),
     )(fields, block_owner.reshape(1, count), ice_covered.reshape(1, count), land_mask)
 

time: 48.5 us -> 43.5 us (0.90)
  Pallas kernels: 44.8 us -> 41.6 us
  local copies, waits for them, and re-layouts: 3.46 us -> 1.67 us
    pallas_call x1, Pallas kernels: 44.8 us -> 41.6 us  [per_device_kernel(): pl.pallas_call(functools.partial(step_kernel, n_lat, n_lon), out_shape=ja...]
    unnamed x9 -> x1, local copies, waits for them, and re-layouts: 3.46 us -> 1.67 us
where the time goes in v2:
time: 43.5 us; the launch traced here: 43.3 us
  Pallas kernels  41.6 us (96%)
  local copies, waits for them, and re-layouts  1.67 us (4%)
    pallas_call x1, Pallas kernels, per_device_kernel(): pl.pallas_call(functools.partial(step_kernel, n_lat, n_lon), out_shape=ja...  41.6 us
    unnamed x1, local copies, waits for them, and re-layouts  1.67 us

profile of v2, /device:TPU:0, one launch (start us, length us, event | category | flops | bytes accessed | tf_op | source)
XLA Modules:
  0.0 43.3 jit_solution(10060586717896494863)
XLA Ops:
  0.0 41.6 %shard_map.46 = f32[1,2,128,256]{3,2,1,0:T(8,128)} custom-call(f32[1,7,128,256]{3,2,1,0:T(8,128)} %fields.1, s32[1,128]{1,0:T(1,128)} %bitcast.2, s32[1,128]{1,0:T(1,128)} %bitcast.3, s32[128,256]{1,0:T(8,128)} %land.1), custom_call_target="tpu_custom_call" | custom-call | tf_op jit(solution)/shard_map/pallas_call | solution.py:642
  41.6 1.7 %copy.6 = f32[1,2,128,256]{3,2,1,0:T(8,128)} copy(f32[1,2,128,256]{3,2,1,0:T(8,128)} %shard_map.46) | data formatting | bytes 524288

commit v3 on v2

--- a/solution.py
+++ b/solution.py
@@ -195,7 +195,7 @@
 
 
 LEAD = 16
-GROUP = 3
+GROUP = 6
 TILE = 8
 MESH = pl.DeviceIdType.MESH
 DIRECTIONS = [(a, b) for a in (-1, 0, 1) for b in (-1, 0, 1) if (a, b) != (0, 0)]
@@ -250,7 +250,7 @@
 
     def each_peer(body):
         def step(k, carry):
-            body((me + peers // 2 + k) % peers)
+            body((me + k) % peers)
             return carry
         lax.fori_loop(0, peers, step, 0)
 
@@ -587,8 +587,6 @@
             for y in range(2):
                 part = both[:, y * width:(y + 1) * width]
                 grid[PUSH_X + c, y, core, main] = grid[MASS, y, core, main] * part
-        halo(CUR_X, 2, pack_mid, got_mid, mid_ssem, mid_rsem, False)
-        unpack(CUR_X, 2, got_mid, lambda r: None)
         wait_bytes(recv.at[pl.ds(0, 2)], fwd_rsem.at[1])
         for c in range(2):
             both = split_dot(perm, recv[c], (0,))
@@ -605,6 +603,8 @@
             back[2, :, pl.ds(y * width, width)] = split_dot(perm, share, (1,))
         send_rows(0, back, 2, 1, ret, 2, ret_ssem.at[0], ret_rsem.at[0])
 
+        halo(CUR_X, 2, pack_mid, got_mid, mid_ssem, mid_rsem, False)
+        unpack(CUR_X, 2, got_mid, lambda r: None)
         halo(PUSH_X, 2, pack_late, got_late, late_ssem, late_rsem, False)
         unpack(PUSH_X, 2, got_late, lambda r: None)
         tile_loop(groups, 1, lambda g: sweep(g, False, True))

time: 43.5 us -> 36.4 us (0.84)
  Pallas kernels: 41.6 us -> 34.6 us
    pallas_call x1, Pallas kernels: 41.6 us -> 34.6 us  [per_device_kernel(): pl.pallas_call(functools.partial(step_kernel, n_lat, n_lon), out_shape=ja...]
where the time goes in v3:
time: 36.4 us; the launch traced here: 36.3 us
  Pallas kernels  34.6 us (95%)
  local copies, waits for them, and re-layouts  1.67 us (5%)
    pallas_call x1, Pallas kernels, per_device_kernel(): pl.pallas_call(functools.partial(step_kernel, n_lat, n_lon), out_shape=ja...  34.6 us
    unnamed x1, local copies, waits for them, and re-layouts  1.67 us

profile of v3, /device:TPU:0, one launch (start us, length us, event | category | flops | bytes accessed | tf_op | source)
XLA Modules:
  0.0 36.3 jit_solution(8486791543989950392)
XLA Ops:
  0.0 34.6 %shard_map.46 = f32[1,2,128,256]{3,2,1,0:T(8,128)} custom-call(f32[1,7,128,256]{3,2,1,0:T(8,128)} %fields.1, s32[1,128]{1,0:T(1,128)} %bitcast.2, s32[1,128]{1,0:T(1,128)} %bitcast.3, s32[128,256]{1,0:T(8,128)} %land.1), custom_call_target="tpu_custom_call" | custom-call | tf_op jit(solution)/shard_map/pallas_call | solution.py:642
  34.6 1.7 %copy.6 = f32[1,2,128,256]{3,2,1,0:T(8,128)} copy(f32[1,2,128,256]{3,2,1,0:T(8,128)} %shard_map.46) | data formatting | bytes 524288
